TPU v7x, 32 devices: a whole 2x2x4 slice. The times are simulated.
32 devices in a mesh: dp: 8 (over y, x, core), mp: 4 (over z).
Axes of the slice: x: 2, y: 2, z: 4, core: 2. Of those that a mesh axis runs over, the one named last changes fastest.
Arguments:
- block_input: bfloat16 [192, 196, 512], P('dp'), may hold values from -6 to 6
- out_grad: bfloat16 [192, 196, 512], P('dp'), may hold values from -6 to 6
- norm_gains: bfloat16 [512, 2], P('dp'), may hold values from 0.5 to 1.5
- offsets: bfloat16 [512, 4], P('dp'), may hold values from -3 to 3
- qkv_weight: bfloat16 [512, 3, 512], P('dp', None, 'mp'), may hold values from -2 to 2
- qv_bias: bfloat16 [2, 512], P(None, 'mp'), may hold values from -3 to 3
- pos_table: float32 [16, 169], P('mp'), may hold values from -4 to 4
- proj_weight: bfloat16 [512, 512], P('dp', 'mp'), may hold values from -0.75 to 0.75
- fc1_weight: bfloat16 [512, 2048], P('dp', 'mp'), may hold values from -0.25 to 0.25
- fc1_bias: bfloat16 [2048], P('mp'), may hold values from -3 to 3
- fc2_weight: bfloat16 [512, 2048], P('dp', 'mp'), may hold values from -0.125 to 0.125
- rel_index: int32 [49, 49], replicated, may hold values from 0 to 168
- region_ids: int32 [14, 14], replicated, may hold values from 0 to 3
Outputs:
- block_output: bfloat16 [192, 196, 512], P('dp')
- input_grad: bfloat16 [192, 196, 512], P('dp')
- norm_gains_grad: float32 [512, 2], P('dp')
- offsets_grad: float32 [512, 4], P('dp')
- qkv_weight_grad: float32 [512, 3, 512], P('dp', None, 'mp')
- qv_bias_grad: float32 [2, 512], P(None, 'mp')
- pos_table_grad: float32 [16, 169], P('mp')
- proj_weight_grad: float32 [512, 512], P('dp', 'mp')
- fc1_weight_grad: float32 [512, 2048], P('dp', 'mp')
- fc1_bias_grad: float32 [2048], P('mp')
- fc2_weight_grad: float32 [512, 2048], P('dp', 'mp')
All inputs are finite; a program needn't handle non-finite values.
Results may differ from a plain program's by a relative error of at most 0.04.
The roundings to bfloat16 on the way count: a program that leaves them out, or rounds other values in their place, can miss the bound.
Values may be sent and summed in bfloat16 or wider, within the bound.
A program may use at most 256 MiB of HBM per device.

v0:
```python
import math
import jax
import jax.numpy as jnp
from jax import lax
from jax.sharding import PartitionSpec as P

D = 512
HD = 32
WIN = 7
SHIFT = 3
SIDE = 14
TOK_IMG = 196


def window_order(tokens_in):
    image_count, channels = (tokens_in.shape[0], tokens_in.shape[-1])
    side_wins = SIDE // WIN
    grid_view = jnp.roll(
        tokens_in.reshape(image_count, SIDE, SIDE, channels), (-SHIFT, -SHIFT), axis=(1, 2)
    )
    grid_view = grid_view.reshape(image_count, side_wins, WIN, side_wins, WIN, channels).transpose(
        0, 1, 3, 2, 4, 5
    )
    return grid_view.reshape(image_count, SIDE * SIDE, channels)


def grid_order(tokens_in):
    image_count, channels = (tokens_in.shape[0], tokens_in.shape[-1])
    side_wins = SIDE // WIN
    grid_view = tokens_in.reshape(image_count, side_wins, side_wins, WIN, WIN, channels).transpose(
        0, 1, 3, 2, 4, 5
    )
    grid_view = jnp.roll(
        grid_view.reshape(image_count, SIDE, SIDE, channels), (SHIFT, SHIFT), axis=(1, 2)
    )
    return grid_view.reshape(image_count, SIDE * SIDE, channels)


def layer_norm(values, gain_col, shift_col):
    row_mean = jnp.mean(values, axis=-1, keepdims=True)
    centred = values - row_mean
    variance = jnp.mean(centred * centred, axis=-1, keepdims=True)
    inv_std = lax.rsqrt(variance + 1e-05)
    normed = centred * inv_std
    return (normed, inv_std, normed * gain_col + shift_col)


def norm_back(grad_out, normed, inv_std, gain_col):
    scaled = grad_out * gain_col
    return inv_std * (
        scaled
        - jnp.mean(scaled, axis=-1, keepdims=True)
        - normed * jnp.mean(scaled * normed, axis=-1, keepdims=True)
    )


def gelu_parts(pre_act):
    cdf_val = 0.5 * (1.0 + jax.scipy.special.erf(pre_act * (1.0 / math.sqrt(2.0))))
    density = jnp.exp(-0.5 * pre_act * pre_act) * (1.0 / math.sqrt(2.0 * math.pi))
    return (pre_act * cdf_val, cdf_val + pre_act * density)


def window_terms(table_rows, rel_index, region_ids, block_size):
    table_len = table_rows.shape[1]
    win_pos = rel_index.shape[0]
    one_hot = (
        rel_index.reshape(-1)[:, None] == jnp.arange(table_len, dtype=jnp.int32)[None, :]
    ).astype(jnp.float32)
    pos_bias = jnp.dot(table_rows, one_hot.T, precision=lax.Precision.HIGHEST).reshape(
        -1, win_pos, win_pos
    )
    side_wins = SIDE // WIN
    labels = (
        region_ids.reshape(side_wins, WIN, side_wins, WIN)
        .transpose(0, 2, 1, 3)
        .reshape(side_wins * side_wins, win_pos)
    )
    penalty = jnp.where(labels[:, :, None] == labels[:, None, :], 0.0, -100.0).astype(jnp.float32)
    win_bias = pos_bias[None] + penalty[:, None]
    return (jnp.tile(win_bias, (block_size, 1, 1, 1)), one_hot)


def blocked():
    for block_size in range(12, 0, -1):
        return block_size
    return 1


def along_rows(left_mat, right_mat):
    return lax.dot_general(
        left_mat, right_mat, (((0,), (0,)), ((), ())), preferred_element_type=jnp.float32
    )


def along_cols(left_mat, right_mat):
    return lax.dot_general(
        left_mat, right_mat, (((1,), (1,)), ((), ())), preferred_element_type=jnp.float32
    )


def attend(queries, key_rows, values, win_bias):
    scores = (
        jnp.einsum("bqhc,bkhc->bhqk", queries, key_rows, preferred_element_type=jnp.float32)
        + win_bias
    )
    row_max = jnp.max(scores, axis=-1, keepdims=True)
    weights_raw = jnp.exp(scores - row_max)
    row_total = jnp.sum(weights_raw, axis=-1, keepdims=True)
    probs = (weights_raw / row_total).astype(jnp.bfloat16)
    attn_rows = jnp.einsum(
        "bhqk,bkhc->bqhc", probs, values, preferred_element_type=jnp.float32
    ).astype(jnp.bfloat16)
    return (attn_rows, (row_max + jnp.log(row_total))[..., 0])


def attend_back(queries, key_rows, values, attn_rows, grad_attn, log_total, win_bias, score_scale):
    scores = (
        jnp.einsum("bqhc,bkhc->bhqk", queries, key_rows, preferred_element_type=jnp.float32)
        + win_bias
    )
    probs = jnp.exp(scores - log_total[..., None])
    grad_probs = jnp.einsum(
        "bqhc,bkhc->bhqk", grad_attn, values, preferred_element_type=jnp.float32
    )
    delta = jnp.sum(
        grad_attn.astype(jnp.float32) * attn_rows.astype(jnp.float32), axis=-1
    ).transpose(0, 2, 1)
    grad_scores = probs * (grad_probs - delta[..., None])
    grad_sb = grad_scores.astype(jnp.bfloat16)
    grad_q = (
        jnp.einsum("bhqk,bkhc->bqhc", grad_sb, key_rows, preferred_element_type=jnp.float32)
        * score_scale
    )
    grad_k = jnp.einsum("bhqk,bqhc->bkhc", grad_sb, queries, preferred_element_type=jnp.float32)
    grad_v = jnp.einsum(
        "bhqk,bqhc->bkhc", probs.astype(jnp.bfloat16), grad_attn, preferred_element_type=jnp.float32
    )
    table_part = jnp.sum(grad_scores, axis=0)
    return (grad_q, grad_k, grad_v, table_part)


def fetch_weights(norm_gains, offsets, qkv_weight, proj_weight, fc1_weight, fc2_weight):
    return (
        lax.all_gather(norm_gains, "dp", axis=0, tiled=True),
        lax.all_gather(offsets, "dp", axis=0, tiled=True),
        lax.all_gather(qkv_weight, "dp", axis=0, tiled=True),
        lax.all_gather(proj_weight, "dp", axis=0, tiled=True),
        lax.all_gather(fc1_weight, "dp", axis=0, tiled=True),
        lax.all_gather(fc2_weight, "dp", axis=0, tiled=True),
    )


def shards(
    block_input,
    out_grad,
    norm_gains,
    offsets,
    qkv_weight,
    qv_bias,
    pos_table,
    proj_weight,
    fc1_weight,
    fc1_bias,
    fc2_weight,
    rel_index,
    region_ids,
):
    win_pos = rel_index.shape[0]
    win_count = TOK_IMG // win_pos
    score_scale = HD ** (-0.5)
    image_count = block_input.shape[0]
    row_count = image_count * TOK_IMG
    heads_here = pos_table.shape[0]
    head_cols = heads_here * HD
    block_size = blocked()
    block_count = image_count // block_size
    win_bias, one_hot = window_terms(pos_table, rel_index, region_ids, block_size)

    def split_heads(flat_rows):
        return flat_rows.reshape(block_count, block_size * win_count, win_pos, heads_here, HD)

    def forward_block(operands):
        return attend(operands[0], operands[1], operands[2], win_bias)

    def backward_block(operands):
        return attend_back(
            operands[0],
            operands[1],
            operands[2],
            operands[3],
            operands[4],
            operands[5],
            win_bias,
            score_scale,
        )

    def gather_all():
        fetched = tuple(
            fetch_weights(norm_gains, offsets, qkv_weight, proj_weight, fc1_weight, fc2_weight)
        )
        return fetched + (qv_bias, fc1_bias)

    gains_w, offsets_w, qkv_w, proj_w, fc1_w, fc2_w, pair_bias, hidden_bias = gather_all()
    gain_cols = gains_w.astype(jnp.float32)
    offset_cols = offsets_w.astype(jnp.float32)
    bias_qv = pair_bias.astype(jnp.float32)
    x_zero = window_order(block_input).reshape(row_count, D).astype(jnp.float32)
    normed1, inv_std1, pre_one = layer_norm(x_zero, gain_cols[:, 0], offset_cols[:, 0])
    h_one = pre_one.astype(jnp.bfloat16)
    qkv_all = jnp.dot(
        h_one, qkv_w.reshape(D, 3 * head_cols), preferred_element_type=jnp.float32
    ).reshape(row_count, 3, head_cols)
    queries = ((qkv_all[:, 0] + bias_qv[0]) * score_scale).astype(jnp.bfloat16)
    key_rows = qkv_all[:, 1].astype(jnp.bfloat16)
    values = (qkv_all[:, 2] + bias_qv[1]).astype(jnp.bfloat16)
    attn_rows, log_total = lax.map(
        forward_block, (split_heads(queries), split_heads(key_rows), split_heads(values))
    )
    attn_flat = attn_rows.reshape(row_count, head_cols)
    attn_out = lax.psum(along_cols(attn_flat, proj_w).astype(jnp.bfloat16), "mp").astype(
        jnp.float32
    )
    x_one = x_zero + attn_out + offset_cols[:, 1]
    normed2, inv_std2, pre_two = layer_norm(x_one, gain_cols[:, 1], offset_cols[:, 2])
    h_two = pre_two.astype(jnp.bfloat16)
    pre_act = jnp.dot(h_two, fc1_w, preferred_element_type=jnp.float32) + hidden_bias.astype(
        jnp.float32
    )
    act_val, act_slope = gelu_parts(pre_act)
    act_rows = act_val.astype(jnp.bfloat16)
    mlp_out = lax.psum(along_cols(act_rows, fc2_w).astype(jnp.bfloat16), "mp").astype(jnp.float32)
    block_rows = (x_one + mlp_out + offset_cols[:, 3]).astype(jnp.bfloat16)
    out_images = grid_order(block_rows.reshape(image_count, TOK_IMG, D))
    gains_w, offsets_w, qkv_w, proj_w, fc1_w, fc2_w, pair_bias, hidden_bias = gather_all()
    gain_cols = gains_w.astype(jnp.float32)
    offset_cols = offsets_w.astype(jnp.float32)
    grad_y = window_order(out_grad).reshape(row_count, D)
    grad_yf = grad_y.astype(jnp.float32)
    grad_fc2b = jnp.sum(grad_yf, axis=0)
    grad_fc2 = along_rows(grad_y, act_rows)
    grad_pre = jnp.dot(grad_y, fc2_w, preferred_element_type=jnp.float32) * act_slope
    grad_preb = grad_pre.astype(jnp.bfloat16)
    grad_fc1 = along_rows(h_two, grad_preb)
    grad_fc1b = jnp.sum(grad_pre, axis=0)
    grad_h2 = lax.psum(along_cols(grad_preb, fc1_w).astype(jnp.bfloat16), "mp").astype(jnp.float32)
    grad_ln2 = jnp.sum(grad_h2 * normed2, axis=0)
    grad_ln2b = jnp.sum(grad_h2, axis=0)
    grad_x1 = grad_yf + norm_back(grad_h2, normed2, inv_std2, gain_cols[:, 1])
    grad_x1b = grad_x1.astype(jnp.bfloat16)
    grad_proj = along_rows(grad_x1b, attn_flat)
    grad_projb = jnp.sum(grad_x1, axis=0)
    grad_attn = jnp.dot(grad_x1b, proj_w, preferred_element_type=jnp.float32).astype(jnp.bfloat16)
    grad_q, grad_k, grad_v, table_part = lax.map(
        backward_block,
        (
            split_heads(queries),
            split_heads(key_rows),
            split_heads(values),
            split_heads(attn_flat),
            split_heads(grad_attn),
            log_total,
        ),
    )
    grad_q = grad_q.reshape(row_count, head_cols)
    grad_k = grad_k.reshape(row_count, head_cols)
    grad_v = grad_v.reshape(row_count, head_cols)
    grad_qv = jnp.stack([jnp.sum(grad_q, axis=0), jnp.sum(grad_v, axis=0)])
    grad_qkv = (
        jnp.stack([grad_q, grad_k, grad_v], axis=1)
        .astype(jnp.bfloat16)
        .reshape(row_count, 3 * head_cols)
    )
    grad_qkvw = along_rows(h_one, grad_qkv).reshape(D, 3, head_cols)
    grad_h1 = lax.psum(
        along_cols(grad_qkv, qkv_w.reshape(D, 3 * head_cols)).astype(jnp.bfloat16), "mp"
    ).astype(jnp.float32)
    grad_ln1 = jnp.sum(grad_h1 * normed1, axis=0)
    grad_ln1b = jnp.sum(grad_h1, axis=0)
    grad_x0 = grad_x1 + norm_back(grad_h1, normed1, inv_std1, gain_cols[:, 0])
    input_share = grid_order(grad_x0.astype(jnp.bfloat16).reshape(image_count, TOK_IMG, D))
    table_grad = jnp.dot(
        jnp.sum(table_part, axis=0).reshape(heads_here, -1),
        one_hot,
        precision=lax.Precision.HIGHEST,
    )
    gains_grad = jnp.stack([grad_ln1, grad_ln2], axis=1)
    offsets_grad = jnp.stack([grad_ln1b, grad_projb, grad_ln2b, grad_fc2b], axis=1)
    grad_qv, table_grad, grad_fc1b = lax.psum((grad_qv, table_grad, grad_fc1b), "dp")
    gains_grad, offsets_grad, grad_qkvw, grad_proj, grad_fc1, grad_fc2 = (
        lax.psum_scatter(
            gains_grad.astype(jnp.bfloat16), "dp", scatter_dimension=0, tiled=True
        ).astype(jnp.float32),
        lax.psum_scatter(
            offsets_grad.astype(jnp.bfloat16), "dp", scatter_dimension=0, tiled=True
        ).astype(jnp.float32),
        lax.psum_scatter(
            grad_qkvw.astype(jnp.bfloat16), "dp", scatter_dimension=0, tiled=True
        ).astype(jnp.float32),
        lax.psum_scatter(
            grad_proj.astype(jnp.bfloat16), "dp", scatter_dimension=0, tiled=True
        ).astype(jnp.float32),
        lax.psum_scatter(
            grad_fc1.astype(jnp.bfloat16), "dp", scatter_dimension=0, tiled=True
        ).astype(jnp.float32),
        lax.psum_scatter(
            grad_fc2.astype(jnp.bfloat16), "dp", scatter_dimension=0, tiled=True
        ).astype(jnp.float32),
    )
    return (
        out_images,
        input_share,
        gains_grad,
        offsets_grad,
        grad_qkvw,
        grad_qv,
        table_grad,
        grad_proj,
        grad_fc1,
        grad_fc1b,
        grad_fc2,
    )


def solution(mesh):
    in_specs = (
        P("dp", None, None),
        P("dp", None, None),
        P("dp", None),
        P("dp", None),
        P("dp", None, "mp"),
        P(None, "mp"),
        P("mp", None),
        P("dp", "mp"),
        P("dp", "mp"),
        P("mp"),
        P("dp", "mp"),
        P(),
        P(),
    )
    out_specs = (
        P("dp", None, None),
        P("dp", None, None),
        P("dp", None),
        P("dp", None),
        P("dp", None, "mp"),
        P(None, "mp"),
        P("mp", None),
        P("dp", "mp"),
        P("dp", "mp"),
        P("mp"),
        P("dp", "mp"),
    )
    return jax.shard_map(shards, mesh=mesh, in_specs=in_specs, out_specs=out_specs, check_vma=False)
```

profile of v0, /device:TPU:0, one launch (start us, length us, event | category | flops | bytes accessed | tf_op | source)
XLA Modules:
  0.0 1215.3 jit_solution(2443523745431153764)
XLA Ops:
  12.8 10.3 all-gather
  72.2 9.7 all_gather.26
  104.2 10.7 squeeze.33
  121.1 10.7 squeeze.34
  138.2 21.6 %while.30 = (s32[]{:T(128)}, bf16[2,48,49,4,32]{2,4,3,1,0:T(8,128)(2,1)}, f32[2,48,4,49]{3,2,1,0:T(4,128)S(1)}, bf16[2,48,49,4,32]{2,4,3,1,0:T(8,128)(2,1)}, bf1...) while((s32[]{:T(128)}, ...), condition=%wide.region_5.6_spmd.clone, body=%wide.region_2.5_spmd.clone.sunk | while | flops 63447552 | bytes 31814608 | solution.py:216
  200.1 9.7 copy.101
  209.8 11.5 reshape.259
  221.3 9.9 all_gather.27
  231.2 11.0 all_gather.28
  242.2 109.5 %all-reduce.6.cloned.1.call-done = bf16[4704,512]{1,0:T(8,128)(2,1)} async-done(((bf16[4704,512]{1,0:T(8,128)(2,1)}), bf16[4704,512]{1,0:T(8,128)(2,1)}) %all-reduce.6.cloned.1.call-update) | async-done | bytes 4816912 | tf_op jit(solution)/shard_map/psum | solution.py:220
  351.7 10.0 fusion.98
  377.5 9.0 fusion.103
  408.3 159.2 %all-reduce.8.cloned.1.call-done = bf16[4704,512]{1,0:T(8,128)(2,1)} async-done(((bf16[4704,512]{1,0:T(8,128)(2,1)}), bf16[4704,512]{1,0:T(8,128)(2,1)}) %all-reduce.8.cloned.1.call-update) | async-done | bytes 4816912 | tf_op jit(solution)/shard_map/psum | solution.py:245
  567.5 10.3 fusion.53
  607.9 42.0 %while.31 = (s32[]{:T(128)}, f32[2,48,49,4,32]{2,4,3,1,0:T(8,128)}, bf16[2,48,49,4,32]{2,4,3,1,0:T(8,128)(2,1)}, f32[2,48,49,4,32]{2,4,3,1,0:T(8,128)}, f32[2,4,...) while((s32[]{:T(128)}, f32[2,48,49,4,32]{2,4,3,1,0:T(8,128)}, ...), condition=%wide.region_16.17_spmd.clone, body=%wide.region_13.16_spmd.clone.sunk | while | flops 153152640 | bytes 111455464 | solution.py:253
  649.9 10.1 copy.137
  666.6 10.1 copy.139
  738.2 14.4 %all-reduce = (f32[2,128]{1,0:T(2,128)}, f32[4,169]{1,0:T(4,128)}, f32[512]{0:T(512)}) all-reduce(f32[2,128]{1,0:T(2,128)S(1)} %pad_maximum_fusion.9, f32[4,169]{1,0:T(4,128)S(1)} %fusion.73, f32[512]{0:T(512)S(1)} %copy-done.48), channel_id=1, replica_groups=mesh['dp'=8,'mp'=4] {'dp'}, use_global_device_ids=true, to_apply=%region_31.32 | all-reduce | flops 1444 | bytes 11552 | tf_op jit(solution)/shard_map/psum | solution.py:288
  754.0 19.0 %reduce-scatter.11.cloned.1.call-done = bf16[64,3,128]{2,0,1:T(8,128)(2,1)} async-done(((bf16[512,3,128]{2,0,1:T(8,128)(2,1)}), bf16[64,3,128]{2,0,1:T(8,128)(2,1)}) %reduce-scatter.11.cloned.1.call-update) | async-done | bytes 49168 | tf_op jit(solution)/shard_map/reduce_scatter | solution.py:296
  774.5 332.8 %all-reduce.10.cloned.1.call-done = (bf16[4704,512]{1,0:T(8,128)(2,1)}, bf16[4704,512]{1,0:T(8,128)(2,1)}) async-done(((bf16[4704,512]{1,0:T(8,128)(2,1)}, bf16[4704,512]{1,0:T(8,128)(2,1)}), (bf16[4704,512]{1,0:T(8,128)(2,1)}, bf16[4704,512]{1,0:T(8,128)(2,1)})) %all-reduce.10.cloned.1.call-update) | async-done | bytes 9633808 | tf_op jit(solution)/shard_map/psum | solution.py:231
  1110.4 10.3 fusion.59
  1121.6 9.2 add_convert_fusion
  1130.8 10.3 fusion.57
  1183.9 23.0 %reduce-scatter.21.cloned.1.call-done = bf16[64,4]{1,0:T(8,128)(2,1)} async-done(((bf16[512,4]{1,0:T(8,128)(2,1)}), bf16[64,4]{1,0:T(8,128)(2,1)}) %reduce-scatter.21.cloned.1.call-update) | async-done | bytes 528
  (338 shorter events, 378.9 us)
Async XLA Ops:
  7.2 63.5 %copy-start = (f32[4,169]{1,0:T(4,128)S(1)}, f32[4,169]{1,0:T(4,128)}, u32[]{:S(2)}) copy-start(f32[4,169]{1,0:T(4,128)} %param.23) | copy-start | bytes 8116
  7.2 344.5 %all-reduce.6.cloned.1.call-start = ((), (), s32[]{:S(2)}) async-start(), calls=%async_computation.6 | async-start | bytes 9633792 | tf_op jit(solution)/shard_map/psum | solution.py:220
  7.3 15.9 %copy-start.49 = (bf16[64,4]{0,1:T(4,128)(2,1)S(1)}, bf16[64,4]{0,1:T(4,128)(2,1)}, u32[]{:S(2)}) copy-start(bf16[64,4]{0,1:T(4,128)(2,1)} %param.20) | copy-start | bytes 1540
  7.3 25.5 %copy-start.37 = (bf16[64,3,128]{2,0,1:T(8,128)(2,1)S(1)}, bf16[64,3,128]{2,0,1:T(8,128)(2,1)}, u32[]{:S(2)}) copy-start(bf16[64,3,128]{2,0,1:T(8,128)(2,1)} %param.21) | copy-start | bytes 147460
  23.2 24.7 %copy-start.38 = (f32[512,1]{0,1:T(1,128)}, f32[512,1]{0,1:T(1,128)S(1)}, u32[]{:S(2)}) copy-start(f32[512,1]{0,1:T(1,128)S(1)} %get-tuple-element.312) | copy-start | bytes 6148
  70.5 18.0 %copy-start.42 = (s32[2401]{0:T(1024)}, s32[2401]{0:T(1024)S(1)}, u32[]{:S(2)}) copy-start(s32[2401]{0:T(1024)S(1)} %eq.34) | copy-start | bytes 28816
  176.1 391.4 %all-reduce.8.cloned.1.call-start = ((), (), s32[]{:S(2)}) async-start(), calls=%async_computation.7 | async-start | bytes 9633792 | tf_op jit(solution)/shard_map/psum | solution.py:245
  209.8 11.5 copy-start.36
  368.2 9.3 slice-start.6
  393.3 330.6 %reduce-scatter.15.cloned.1.call-start = ((), (), s32[]{:S(2)}) async-start(), calls=%async_computation.10 | async-start | bytes 589824 | tf_op jit(solution)/shard_map/reduce_scatter | solution.py:302
  400.8 324.5 %reduce-scatter.17.cloned.1.call-start = ((), (), s32[]{:S(2)}) async-start(), calls=%async_computation.11 | async-start | bytes 589824 | tf_op jit(solution)/shard_map/reduce_scatter | solution.py:305
  408.3 344.4 %reduce-scatter.13.cloned.1.call-start = ((), (), s32[]{:S(2)}) async-start(), calls=%async_computation.9 | async-start | bytes 147456 | tf_op jit(solution)/shard_map/reduce_scatter | solution.py:299
  615.5 8.3 slice-start.2
  636.5 8.3 slice-start.2
  703.6 69.5 %reduce-scatter.11.cloned.1.call-start = ((), (), s32[]{:S(2)}) async-start(), calls=%async_computation.8 | async-start | bytes 442368 | tf_op jit(solution)/shard_map/reduce_scatter | solution.py:296
  710.2 397.0 %all-reduce.10.cloned.1.call-start = ((), (), s32[]{:S(2)}) async-start(), calls=%async_computation.14 | async-start | bytes 19267584 | tf_op jit(solution)/shard_map/psum | solution.py:231
  721.6 460.9 %reduce-scatter.19.cloned.1.call-start = ((), (), s32[]{:S(2)}) async-start(), calls=%async_computation.12 | async-start | bytes 147456
  730.3 7.9 copy-start.48
  733.9 376.5 %copy-start.39 = (f32[512,1]{0,1:T(1,128)S(1)}, f32[512,1]{0,1:T(1,128)}, u32[]{:S(2)}) copy-start(f32[512,1]{0,1:T(1,128)} %copy-done.38) | copy-start | bytes 6148
  1110.3 11.3 copy-start.44
  1110.4 20.5 %slice-start = ((s8[4816896]{0:T(1024)(128)(4,1)}), s8[622592]{0:T(1024)(128)(4,1)S(1)}, s32[]{:S(2)}) async-start(s8[4816896]{0:T(1024)(128)(4,1)} %bitcast.240), calls=%async_computation.15 | async-start | bytes 1245184
  1121.6 85.4 %reduce-scatter.21.cloned.1.call-start = ((), (), s32[]{:S(2)}) async-start(), calls=%async_computation.13 | async-start | bytes 147456
  1121.6 9.2 slice-start.1
  1174.2 34.1 %copy-start.1 = (f32[4,169]{1,0:T(4,128)S(1)}, f32[4,169]{1,0:T(4,128)}, u32[]{:S(2)}) copy-start(f32[4,169]{1,0:T(4,128)} %param.23) | copy-start | bytes 8116
  (63 other events, 265.2 us)
Sparse Core Ops, SparseCore 0:
  176.2 175.3 all-reduce.5
  393.4 174.0 all-reduce.7
  570.6 33.0 reduce-scatter.14
  606.6 34.1 reduce-scatter.16
  703.7 32.4 reduce-scatter.12
  739.1 33.8 reduce-scatter.10
  776.2 331.0 all-reduce.9
  1121.7 32.5 reduce-scatter.18
  1174.3 32.5 reduce-scatter.20
where the time goes:
time: 1230 us; the launch traced here: 1220 us
  waiting for transfers between devices  644 us (52%)
  local copies, waits for them, and re-layouts  245 us (20%)
  other arithmetic  129 us (10%)
  matrix products  109 us (9%)
  blocking collectives  72.7 us (6%)
  between operations  15.1 us (1%)
    psum x1, waiting for transfers between devices, shards(): lax.psum(along_cols(act_rows, fc2_w).astype(jnp.bfloat16), 'mp')  333 us
    psum x1, waiting for transfers between devices, shards(): lax.psum(along_cols(grad_preb, fc1_w).astype(jnp.bfloat16), 'mp')  159 us
    psum x1, waiting for transfers between devices, shards(): lax.psum(along_cols(attn_flat, proj_w).astype(jnp.bfloat16), 'mp')  109 us
    another operation x6, local copies, waits for them, and re-layouts, shards(): jnp.stack([grad_q, grad_k, grad_v], axis=1).astype(jnp.bfloat16)  47.6 us
    unnamed x101, local copies, waits for them, and re-layouts  35.7 us
    dot_general x4, matrix products, along_rows(): lax.dot_general(left_mat, right_mat, (((0,), (0,)), ((), ())), preferred_...  27.4 us
  transfers between devices with their start and end apart: 9, of which 5 were waited for; matrix products, arithmetic and copies ran while one was open for 23% of the time, Pallas kernels for 0%

commit v1 on v0

--- a/solution.py
+++ b/solution.py
@@ -228,7 +228,9 @@
     )
     act_val, act_slope = gelu_parts(pre_act)
     act_rows = act_val.astype(jnp.bfloat16)
-    mlp_out = lax.psum(along_cols(act_rows, fc2_w).astype(jnp.bfloat16), "mp").astype(jnp.float32)
+    mlp_out = jnp.sum(
+        lax.all_gather(along_cols(act_rows, fc2_w).astype(jnp.bfloat16), "mp"), axis=0
+    ).astype(jnp.float32)
     block_rows = (x_one + mlp_out + offset_cols[:, 3]).astype(jnp.bfloat16)
     out_images = grid_order(block_rows.reshape(image_count, TOK_IMG, D))
     gains_w, offsets_w, qkv_w, proj_w, fc1_w, fc2_w, pair_bias, hidden_bias = gather_all()

time: 1230 us -> 1390 us (1.13)
  waiting for transfers between devices: 644 us -> 792 us
    all_gather x0 -> x1, waiting for transfers between devices: none -> 319 us  [shards(): lax.all_gather(along_cols(act_rows, fc2_w).astype(jnp.bfloat16), 'mp')]
    psum x1, waiting for transfers between devices: 333 us -> 176 us  [shards(): lax.psum(along_cols(grad_qkv, qkv_w.reshape(D, 3 * head_cols)).astype(jnp...]
    reduce_scatter x1, waiting for transfers between devices: 19 us -> 2.11 us  [shards(): lax.psum_scatter(grad_qkvw.astype(jnp.bfloat16), 'dp', scatter_dimension=...]
    unnamed x11 -> x12, waiting for transfers between devices: 23.1 us -> 33.9 us
    unnamed x101 -> x89, local copies, waits for them, and re-layouts: 35.7 us -> 35.8 us
  transfers between devices with their start and end apart: 9 -> 10, of which waited for: 5 -> 6; matrix products, arithmetic and copies ran while one was open for 23% -> 22% of each run, Pallas kernels for 0% -> 0%
where the time goes in v1:
time: 1390 us; the launch traced here: 1380 us
  waiting for transfers between devices  792 us (57%)
  local copies, waits for them, and re-layouts  245 us (18%)
  other arithmetic  140 us (10%)
  matrix products  112 us (8%)
  blocking collectives  72.6 us (5%)
  between operations  15 us (1%)
    all_gather x1, waiting for transfers between devices, shards(): lax.all_gather(along_cols(act_rows, fc2_w).astype(jnp.bfloat16), 'mp')  319 us
    psum x1, waiting for transfers between devices, shards(): lax.psum(along_cols(grad_qkv, qkv_w.reshape(D, 3 * head_cols)).astype(jnp...  176 us
    psum x1, waiting for transfers between devices, shards(): lax.psum(along_cols(grad_preb, fc1_w).astype(jnp.bfloat16), 'mp')  151 us
    psum x1, waiting for transfers between devices, shards(): lax.psum(along_cols(attn_flat, proj_w).astype(jnp.bfloat16), 'mp')  110 us
    another operation x6, local copies, waits for them, and re-layouts, shards(): jnp.stack([grad_q, grad_k, grad_v], axis=1).astype(jnp.bfloat16)  47.7 us
    unnamed x89, local copies, waits for them, and re-layouts  35.8 us
    unnamed x12, waiting for transfers between devices  33.9 us
  transfers between devices with their start and end apart: 10, of which 6 were waited for; matrix products, arithmetic and copies ran while one was open for 22% of the time, Pallas kernels for 0%

profile of v1, /device:TPU:0, one launch (start us, length us, event | category | flops | bytes accessed | tf_op | source)
XLA Modules:
  0.0 1379.0 jit_solution(2786264535985791960)
XLA Ops:
  12.8 10.3 all-gather.1
  72.2 9.5 all_gather.32
  104.0 10.7 squeeze.33
  121.0 10.7 squeeze.34
  138.1 21.8 %while.30 = (s32[]{:T(128)}, bf16[2,48,49,4,32]{2,4,3,1,0:T(8,128)(2,1)}, f32[2,48,4,49]{3,2,1,0:T(4,128)S(1)}, bf16[2,48,49,4,32]{2,4,3,1,0:T(8,128)(2,1)}, bf1...) while((s32[]{:T(128)}, ...), condition=%wide.region_5.6_spmd.clone, body=%wide.region_2.5_spmd.clone.sunk | while | flops 63447552 | bytes 31814608 | solution.py:216
  199.9 9.8 copy.101
  209.7 11.5 reshape.259
  221.2 9.9 all_gather.33
  231.1 11.0 all_gather.34
  242.0 109.7 %all-reduce.5.cloned.1.call-done = bf16[4704,512]{1,0:T(8,128)(2,1)} async-done(((bf16[4704,512]{1,0:T(8,128)(2,1)}), bf16[4704,512]{1,0:T(8,128)(2,1)}) %all-reduce.5.cloned.1.call-update) | async-done | bytes 4816912 | tf_op jit(solution)/shard_map/psum | solution.py:220
  351.7 10.1 fusion.98
  416.2 151.3 %all-reduce.7.cloned.1.call-done = bf16[4704,512]{1,0:T(8,128)(2,1)} async-done(((bf16[4704,512]{1,0:T(8,128)(2,1)}), bf16[4704,512]{1,0:T(8,128)(2,1)}) %all-reduce.7.cloned.1.call-update) | async-done | bytes 4816912 | tf_op jit(solution)/shard_map/psum | solution.py:247
  567.6 10.3 fusion.53
  578.5 318.7 %all-gather.5.cloned.1.call-done = bf16[18816,512]{1,0:T(8,128)(2,1)} async-done(((bf16[4704,512]{1,0:T(8,128)(2,1)}), bf16[18816,512]{1,0:T(8,128)(2,1)}) %all-gather.5.cloned.1.call-update) | async-done | bytes 19267600 | tf_op jit(solution)/shard_map/all_gather | solution.py:232
  897.2 13.9 %reduce_sum.205 = bf16[4704,512]{1,0:T(8,128)(2,1)} reduce(bf16[4,4704,512]{2,1,0:T(8,128)(2,1)} %bitcast.254, bf16[]{:T(256)} %constant.64.clone.1), dimensions={0}, to_apply=%region_9.10 | reduce | flops 7225344 | bytes 24084482 | tf_op jit(solution)/shard_map/reduce_sum | solution.py:231
  911.0 11.2 fusion.93
  944.4 42.1 %while.31 = (s32[]{:T(128)}, f32[2,48,49,4,32]{2,4,3,1,0:T(8,128)}, bf16[2,48,49,4,32]{2,4,3,1,0:T(8,128)(2,1)}, f32[2,48,49,4,32]{2,4,3,1,0:T(8,128)}, f32[2,4,...) while((s32[]{:T(128)}, f32[2,48,49,4,32]{2,4,3,1,0:T(8,128)}, ...), condition=%wide.region_16.17_spmd.clone, body=%wide.region_13.16_spmd.clone.sunk | while | flops 153152640 | bytes 111455464 | solution.py:255
  986.5 10.1 copy.137
  1003.2 10.1 copy.139
  1086.8 14.4 %all-reduce = (f32[2,128]{1,0:T(2,128)}, f32[4,169]{1,0:T(4,128)}, f32[512]{0:T(512)}) all-reduce(f32[2,128]{1,0:T(2,128)S(1)} %pad_maximum_fusion.9, f32[4,169]{1,0:T(4,128)S(1)} %fusion.73, f32[512]{0:T(512)S(1)} %copy-done.44), channel_id=1, replica_groups=mesh['dp'=8,'mp'=4] {'dp'}, use_global_device_ids=true, to_apply=%region_31.32 | all-reduce | flops 1444 | bytes 11552 | tf_op jit(solution)/shard_map/psum | solution.py:290
  1111.2 176.1 %all-reduce.9.cloned.1.call-done = bf16[4704,512]{1,0:T(8,128)(2,1)} async-done(((bf16[4704,512]{1,0:T(8,128)(2,1)}), bf16[4704,512]{1,0:T(8,128)(2,1)}) %all-reduce.9.cloned.1.call-update) | async-done | bytes 4816912 | tf_op jit(solution)/shard_map/psum | solution.py:276
  1290.4 10.2 fusion.59
  1301.5 11.9 fusion.57
  1336.9 33.7 %reduce-scatter.21.cloned.1.call-done = bf16[64,4]{1,0:T(8,128)(2,1)} async-done(((bf16[512,4]{1,0:T(8,128)(2,1)}), bf16[64,4]{1,0:T(8,128)(2,1)}) %reduce-scatter.21.cloned.1.call-update) | async-done | bytes 528
  (328 shorter events, 388.0 us)
Async XLA Ops:
  7.2 63.5 %copy-start = (f32[4,169]{1,0:T(4,128)S(1)}, f32[4,169]{1,0:T(4,128)}, u32[]{:S(2)}) copy-start(f32[4,169]{1,0:T(4,128)} %param.23) | copy-start | bytes 8116
  7.2 344.5 %all-reduce.5.cloned.1.call-start = ((), (), s32[]{:S(2)}) async-start(), calls=%async_computation.6 | async-start | bytes 9633792 | tf_op jit(solution)/shard_map/psum | solution.py:220
  7.3 15.9 %copy-start.45 = (bf16[64,4]{0,1:T(4,128)(2,1)S(1)}, bf16[64,4]{0,1:T(4,128)(2,1)}, u32[]{:S(2)}) copy-start(bf16[64,4]{0,1:T(4,128)(2,1)} %param.20) | copy-start | bytes 1540
  7.3 25.5 %copy-start.33 = (bf16[64,3,128]{2,0,1:T(8,128)(2,1)S(1)}, bf16[64,3,128]{2,0,1:T(8,128)(2,1)}, u32[]{:S(2)}) copy-start(bf16[64,3,128]{2,0,1:T(8,128)(2,1)} %param.21) | copy-start | bytes 147460
  23.2 24.7 %copy-start.34 = (f32[512,1]{0,1:T(1,128)}, f32[512,1]{0,1:T(1,128)S(1)}, u32[]{:S(2)}) copy-start(f32[512,1]{0,1:T(1,128)S(1)} %get-tuple-element.311) | copy-start | bytes 6148
  70.5 17.9 %copy-start.38 = (s32[2401]{0:T(1024)}, s32[2401]{0:T(1024)S(1)}, u32[]{:S(2)}) copy-start(s32[2401]{0:T(1024)S(1)} %eq.34) | copy-start | bytes 28816
  176.2 391.4 %all-reduce.7.cloned.1.call-start = ((), (), s32[]{:S(2)}) async-start(), calls=%async_computation.7 | async-start | bytes 9633792 | tf_op jit(solution)/shard_map/psum | solution.py:247
  209.7 11.5 copy-start.32
  368.3 9.3 slice-start.4
  393.4 503.8 %all-gather.5.cloned.1.call-start = ((), (), s32[]{:S(2)}) async-start(), calls=%async_computation.13 | async-start | bytes 24084480 | tf_op jit(solution)/shard_map/all_gather | solution.py:232
  400.8 655.1 %reduce-scatter.15.cloned.1.call-start = ((), (), s32[]{:S(2)}) async-start(), calls=%async_computation.11 | async-start | bytes 589824 | tf_op jit(solution)/shard_map/reduce_scatter | solution.py:304
  408.7 648.7 %reduce-scatter.17.cloned.1.call-start = ((), (), s32[]{:S(2)}) async-start(), calls=%async_computation.12 | async-start | bytes 589824 | tf_op jit(solution)/shard_map/reduce_scatter | solution.py:307
  416.2 690.1 %reduce-scatter.13.cloned.1.call-start = ((), (), s32[]{:S(2)}) async-start(), calls=%async_computation.10 | async-start | bytes 147456 | tf_op jit(solution)/shard_map/reduce_scatter | solution.py:301
  897.2 13.9 %copy-start.40 = (f32[512,1]{0,1:T(1,128)S(1)}, f32[512,1]{0,1:T(1,128)}, u32[]{:S(2)}) copy-start(f32[512,1]{0,1:T(1,128)} %get-tuple-element.306) | copy-start | bytes 6148
  951.9 8.2 slice-start
  972.9 6.8 slice-start.2
  973.0 8.3 slice-start
  1013.3 6.9 copy-start.19
  1040.2 69.5 %reduce-scatter.11.cloned.1.call-start = ((), (), s32[]{:S(2)}) async-start(), calls=%async_computation.9 | async-start | bytes 442368 | tf_op jit(solution)/shard_map/reduce_scatter | solution.py:298
  1046.9 240.4 %all-reduce.9.cloned.1.call-start = ((), (), s32[]{:S(2)}) async-start(), calls=%async_computation.8 | async-start | bytes 9633792 | tf_op jit(solution)/shard_map/psum | solution.py:276
  1053.7 281.9 %reduce-scatter.19.cloned.1.call-start = ((), (), s32[]{:S(2)}) async-start(), calls=%async_computation.14 | async-start | bytes 147456
  1106.3 184.1 %copy-start.35 = (f32[512,1]{0,1:T(1,128)S(1)}, f32[512,1]{0,1:T(1,128)}, u32[]{:S(2)}) copy-start(f32[512,1]{0,1:T(1,128)} %copy-done.34) | copy-start | bytes 6148
  1301.5 69.1 %reduce-scatter.21.cloned.1.call-start = ((), (), s32[]{:S(2)}) async-start(), calls=%async_computation.15 | async-start | bytes 147456
  1330.4 41.6 %copy-start.1 = (f32[4,169]{1,0:T(4,128)S(1)}, f32[4,169]{1,0:T(4,128)}, u32[]{:S(2)}) copy-start(f32[4,169]{1,0:T(4,128)} %param.23) | copy-start | bytes 8116
  (58 other events, 219.2 us)
Sparse Core Ops, SparseCore 0:
  176.3 175.3 all-reduce.4
  393.5 174.0 all-reduce.6
  569.2 327.9 all-gather.4
  900.1 32.8 reduce-scatter.14
  936.0 34.1 reduce-scatter.16
  1040.4 32.3 reduce-scatter.12
  1075.8 33.8 reduce-scatter.10
  1112.1 175.1 all-reduce.8
  1301.6 32.4 reduce-scatter.18
  1337.0 33.5 reduce-scatter.20
